TPU v7x, 32 devices: a whole 2x2x4 slice. The times are simulated.
32 devices in a mesh: dp: 8 (over z, y), col: 4 (over x, core).
Axes of the slice: x: 2, y: 2, z: 4, core: 2. Of those that a mesh axis runs over, the one named last changes fastest.
Arguments:
- view_first: bfloat16 [8192, 4096], P('dp'), may hold values from -1000 to 1000
- view_second: bfloat16 [8192, 4096], P('dp', 'col'), may hold values from -1000 to 1000
- valid_rows: int32 [8], P('dp'), may hold values from 1 to 1024, as said below
Outputs:
- correlation: float32 [4096, 4096], P('dp', 'col')
- loss: float32 [], replicated
Inputs may be any that keep to these rules, and one draw needn't show every extreme that they name: `valid_rows`: some micro-batch uses all 1024 rows.
All inputs are finite; a program needn't handle non-finite values.
Results may differ from a plain program's by a relative error of at most 0.0005.
Values sent between devices are 32-bit elements; how exact they have to be, the bound alone decides.
A program may use at most 128 MiB of HBM per device.

v0:
```python
import jax
import jax.numpy as jnp
from jax import lax
from jax.sharding import PartitionSpec as P

epsilon = 1e-05
off_weight = 0.0051


def per_device(view_first, view_second, valid_rows):
    local_rows = view_first.shape[0]
    feature_width = view_first.shape[1]
    column_width = view_second.shape[1]
    group_count = lax.axis_size("dp")
    block_rows = feature_width // group_count
    used_rows = valid_rows[0]
    used_float = used_rows.astype(jnp.float32)
    positions = lax.broadcasted_iota(jnp.int32, (local_rows, 1), 0)
    live_col = (positions < used_rows).astype(jnp.float32)
    live_row = jnp.transpose(live_col).astype(jnp.bfloat16)
    sum_first = jnp.dot(live_row, view_first, preferred_element_type=jnp.float32)[0]
    sum_second = jnp.dot(live_row, view_second, preferred_element_type=jnp.float32)[0]
    mean_first = sum_first / used_float
    mean_second = sum_second / used_float
    centered_first = ((view_first.astype(jnp.float32) - mean_first) * live_col).astype(jnp.bfloat16)
    centered_second = ((view_second.astype(jnp.float32) - mean_second) * live_col).astype(
        jnp.bfloat16
    )
    square_first = jnp.sum(jnp.square(centered_first.astype(jnp.float32)), axis=0)
    square_second = jnp.sum(jnp.square(centered_second.astype(jnp.float32)), axis=0)
    group_index = lax.axis_index("dp")
    row_start = group_index * block_rows
    counts_all, sums_first, sums_second, squares_first, squares_second = (
        lax.all_gather(used_float[None], "dp", axis=0, tiled=True),
        lax.all_gather(sum_first[None], "dp", axis=0, tiled=True),
        lax.all_gather(sum_second[None], "dp", axis=0, tiled=True),
        lax.all_gather(square_first[None], "dp", axis=0, tiled=True),
        lax.all_gather(square_second[None], "dp", axis=0, tiled=True),
    )
    moment = lax.psum_scatter(
        lax.dot_general(
            centered_first,
            centered_second,
            (((0,), (0,)), ((), ())),
            preferred_element_type=jnp.float32,
        ),
        "dp",
        scatter_dimension=0,
        tiled=True,
    )
    counts_col = counts_all[:, None]
    all_rows = jnp.sum(counts_all)
    glob_first = jnp.sum(sums_first, axis=0) / all_rows
    glob_second = jnp.sum(sums_second, axis=0) / all_rows
    shifts_first = sums_first / counts_col - glob_first[None, :]
    shifts_second = sums_second / counts_col - glob_second[None, :]
    owned_shift = lax.dynamic_slice_in_dim(shifts_first, row_start, block_rows, 1)
    owned_square = lax.dynamic_slice_in_dim(squares_first, row_start, block_rows, 1)
    spread_rows = jnp.sum(owned_square + counts_col * jnp.square(owned_shift), axis=0)
    spread_second = jnp.sum(squares_second + counts_col * jnp.square(shifts_second), axis=0)
    weighted = owned_shift * counts_col
    moment = moment + lax.dot_general(
        weighted,
        shifts_second,
        (((0,), (0,)), ((), ())),
        precision=lax.Precision.HIGHEST,
        preferred_element_type=jnp.float32,
    )
    scale_rows = jnp.sqrt(spread_rows / all_rows + epsilon)
    scale_cols = jnp.sqrt(spread_second / all_rows + epsilon)
    correlation = moment / (all_rows * scale_rows[:, None] * scale_cols[None, :])
    col_start = lax.axis_index("col") * column_width
    global_rows = row_start + lax.broadcasted_iota(jnp.int32, (block_rows, 1), 0)
    global_cols = col_start + lax.broadcasted_iota(jnp.int32, (1, column_width), 1)
    diagonal = global_rows == global_cols
    terms = jnp.where(diagonal, jnp.square(1.0 - correlation), off_weight * jnp.square(correlation))
    partial_loss = jnp.sum(terms)
    loss = lax.psum(partial_loss, ("dp", "col")) / feature_width
    return (correlation, loss)


def solution(mesh):
    return jax.shard_map(
        per_device,
        mesh=mesh,
        in_specs=(P("dp", None), P("dp", "col"), P("dp")),
        out_specs=(P("dp", "col"), P()),
        check_vma=False,
    )
```

profile of v0, /device:TPU:0, one launch (start us, length us, event | category | flops | bytes accessed | tf_op | source)
XLA Modules:
  0.0 367.4 jit_solution(4194407191205753321)
XLA Ops:
  7.2 0.0 reduce-scatter.2.cloned.1.call-start
  7.9 0.0 copy-start.1
  7.9 0.0 copy-start
  7.9 4.7 %fusion.7 = f32[1,4096]{1,0:T(1,128)S(1)} fusion(bf16[1024,1]{0,1:T(2,128)(2,1)S(1)} %reshape.67, bf16[1024,4096]{1,0:T(8,128)(2,1)} %param.3), kind=kOutput, calls=%fused_computation.25 | convolution fusion | flops 8388608 | bytes 8407040 | tf_op jit(solution)/shard_map/dot_general | solution.py:21
  12.6 0.0 copy-done.1
  12.6 0.4 fusion.8
  13.0 1.3 copy-done
  14.3 12.8 %fusion = f32[4096,1024]{1,0:T(8,128)} fusion(bf16[1024,4096]{1,0:T(8,128)(2,1)S(1)} %copy-done, f32[1024]{0:T(1024)S(1)} %get-tuple-element.4, f32[4096]{0:T(1024)S(1)} %broadcast_divide_fusion.1, bf16[1024,1024]{1,0:T(8,128)(2,1)S(1)} %copy-done.1, f32[1024]{0:T(1024)S(1)} %broadcast_divide_fusion.3), kind=kOutput, calls=%fused_computation.4 | convolution fusion | flops 8610906112 | bytes 27287552 | tf_op jit(solution)/shard_map/dot_general | solution.py:41
  27.1 0.0 copy-start.2
  27.1 0.0 reduce-scatter.2.cloned.1.call-update
  27.1 0.6 copy-done.2
  27.7 0.6 dynamic-slice
  28.3 0.8 dynamic-update-slice
  29.1 24.4 %all-reduce = f32[8]{0:T(128)S(1)} all-reduce(f32[8]{0:T(128)S(1)} %dynamic-update-slice), channel_id=1, replica_groups=mesh['dp'=8,'col'=4] {'dp'}, use_global_device_ids=true, to_apply=%add | all-reduce | flops 8 | bytes 64
  53.4 0.6 reduce_sum.73
  54.1 32.5 %all-gather = f32[32768]{0:T(1024)S(1)} all-gather(f32[4096]{0:T(1024)S(1)} %bitcast.12), channel_id=2, replica_groups=mesh['dp'=8,'col'=4] {'dp'}, dimensions={0}, use_global_device_ids=true | all-gather | bytes 147456 | tf_op jit(solution)/shard_map/all_gather | solution.py:35
  86.7 6.6 %multiply_reduce_fusion = f32[4096]{0:T(1024)S(1)} fusion(f32[1024]{0:T(1024)S(1)} %get-tuple-element.4, f32[4096]{0:T(1024)S(1)} %broadcast_divide_fusion.1, bf16[1024,4096]{1,0:T(8,128)(2,1)} %param.3), kind=kLoop, calls=%fused_computation | loop fusion | flops 29356032 | bytes 8425472 | tf_op jit(solution)/shard_map/reduce_sum | solution.py:29
  93.2 32.6 %all-gather.2 = f32[32768]{0:T(1024)S(1)} all-gather(f32[4096]{0:T(1024)S(1)} %multiply_reduce_fusion), channel_id=4, replica_groups=mesh['dp'=8,'col'=4] {'dp'}, dimensions={0}, use_global_device_ids=true | all-gather | bytes 147456 | tf_op jit(solution)/shard_map/all_gather | solution.py:37
  125.9 31.9 %all-gather.1 = f32[8192]{0:T(1024)S(1)} all-gather(f32[1024]{0:T(1024)S(1)} %bitcast.14), channel_id=3, replica_groups=mesh['dp'=8,'col'=4] {'dp'}, dimensions={0}, use_global_device_ids=true | all-gather | bytes 36864 | tf_op jit(solution)/shard_map/all_gather | solution.py:36
  157.7 0.7 multiply_reduce_fusion.1
  158.5 31.5 %all-gather.3 = f32[8192]{0:T(1024)S(1)} all-gather(f32[1024]{0:T(1024)S(1)} %multiply_reduce_fusion.1), channel_id=5, replica_groups=mesh['dp'=8,'col'=4] {'dp'}, dimensions={0}, use_global_device_ids=true | all-gather | bytes 36864 | tf_op jit(solution)/shard_map/all_gather | solution.py:38
  190.0 0.7 broadcast_divide_fusion
  190.6 0.1 dynamic-slice.1
  190.7 0.1 add_reduce_fusion.1
  190.8 0.7 broadcast_divide_fusion.2
  191.5 0.1 add_reduce_fusion
  191.6 0.7 sqrt_multiply_fusion
  192.2 0.7 add_sqrt_fusion
  192.9 120.3 %reduce-scatter.2.cloned.1.call-done = f32[512,1024]{1,0:T(8,128)} async-done(((f32[4096,1024]{1,0:T(8,128)}), f32[512,1024]{1,0:T(8,128)}) %reduce-scatter.2.cloned.1.call-update) | async-done | bytes 2097168 | tf_op jit(solution)/shard_map/reduce_scatter | solution.py:40
  313.2 6.1 %select_reduce_fusion = (f32[]{:T(128)}, f32[512,1024]{1,0:T(8,128)}) fusion(s32[1024]{0:T(1024)S(1)} %iota_add_fusion, s32[512]{0:T(512)S(1)} %iota_add_fusion.1, f32[1024]{0:T(1024)S(1)} %add_sqrt_fusion, f32[512]{0:T(512)S(1)} %sqrt_multiply_fusion, f32[512,1024]{1,0:T(8,128)} %reduce-scatter.2.cloned.1.call-done, f32[8,1024]{1,0:T(8,128)S(1)} %reshape.59, ...), kind=kOutput, calls=%fused_computation.5 | convolution fusion | flops 55603200 | bytes 4262920 | tf_op jit(solution)/shard_map/dot_general | solution.py:62
  319.3 39.5 %psum.7 = f32[]{:T(128)} all-reduce(f32[]{:T(128)} %get-tuple-element.2), channel_id=1, replica_groups=mesh['dp'=8,'col'=4] {'dp','col'}, use_global_device_ids=true, to_apply=%region_9.10 | all-reduce | flops 1 | bytes 8 | tf_op jit(solution)/shard_map/psum | solution.py:78
  (13 shorter events, 0.2 us)
Async XLA Ops:
  7.2 306.0 %reduce-scatter.2.cloned.1.call-start = ((), (), s32[]{:S(2)}) async-start(), calls=%async_computation.1 | async-start | bytes 18874368 | tf_op jit(solution)/shard_map/reduce_scatter | solution.py:40
  7.9 4.8 %copy-start.1 = (bf16[1024,1024]{1,0:T(8,128)(2,1)S(1)}, bf16[1024,1024]{1,0:T(8,128)(2,1)}, u32[]{:S(2)}) copy-start(bf16[1024,1024]{1,0:T(8,128)(2,1)} %param.4) | copy-start | bytes 6291460
  7.9 6.4 %copy-start = (bf16[1024,4096]{1,0:T(8,128)(2,1)S(1)}, bf16[1024,4096]{1,0:T(8,128)(2,1)}, u32[]{:S(2)}) copy-start(bf16[1024,4096]{1,0:T(8,128)(2,1)} %param.3) | copy-start | bytes 25165828
  27.1 0.7 copy-start.2
Sparse Core Ops, SparseCore 0:
  27.2 285.9 reduce-scatter.1
where the time goes:
time: 368 us; the launch traced here: 367 us
  blocking collectives  192 us (52%)
  waiting for transfers between devices  120 us (33%)
  matrix products  24 us (7%)
  between operations  16.6 us (5%)
  other arithmetic  10.7 us (3%)
    reduce_scatter x1, waiting for transfers between devices, per_device(): lax.psum_scatter(lax.dot_general(centered_first, centered_second, (((0,),...  120 us
    psum x1, blocking collectives, per_device(): loss = lax.psum(partial_loss, ('dp', 'col')) / feature_width  39.5 us
    all_gather x1, blocking collectives, per_device(): lax.all_gather(square_first[None], 'dp', axis=0, tiled=True)  32.6 us
    all_gather x1, blocking collectives, per_device(): lax.all_gather(sum_first[None], 'dp', axis=0, tiled=True)  32.5 us
    all_gather x1, blocking collectives, per_device(): lax.all_gather(sum_second[None], 'dp', axis=0, tiled=True)  31.9 us
    all_gather x1, blocking collectives, per_device(): lax.all_gather(square_second[None], 'dp', axis=0, tiled=True)  31.5 us
    unnamed x1, blocking collectives  24.4 us
    dot_general x1, matrix products, per_device(): lax.dot_general(centered_first, centered_second, (((0,), (0,)), ((), ()))...  12.8 us
  transfers between devices with their start and end apart: 1, of which 1 were waited for; matrix products, arithmetic and copies ran while one was open for 3% of the time, Pallas kernels for 0%

commit v1 on v0

--- a/solution.py
+++ b/solution.py
@@ -1,10 +1,207 @@
+import functools
 import jax
 import jax.numpy as jnp
 from jax import lax
+from jax.experimental import pallas as pl
+from jax.experimental.pallas import tpu as pltpu
 from jax.sharding import PartitionSpec as P
 
 epsilon = 1e-05
 off_weight = 0.0051
+MESH = pl.DeviceIdType.MESH
+
+
+def owner_at(place, length, step):
+    low = jnp.minimum(place, length - 1 - place)
+    high = length - 1 - low
+    single = high - low
+    rest = step - single
+    upward = jnp.where(step < single, place == low, rest % 2 == 0)
+    reach = jnp.where(step < single, high - step, low - rest // 2)
+    return jnp.where(upward, place + reach, place - reach)
+
+
+def reduce_kernel(
+    n, x_ref, y_ref, st_ref, out_ref, stats_ref,
+    pair_out, own, pair_in, line_in, own_b, line_in_b, swap_in, st_in,
+    pair_ss, pair_rs, line_ss, line_rs, lineb_ss, lineb_rs, swap_ss, swap_rs, st_ss, st_rs,
+):
+    me = lax.axis_index("dp")
+    length = n // 2
+    place, side = me // 2, me % 2
+    twin = place * 2 + (1 - side)
+    rows = x_ref.shape[1]
+    wide = own.shape[2]
+    total = y_ref.shape[1]
+
+    barrier = pltpu.get_barrier_semaphore()
+
+    def greet(k, carry):
+        pl.semaphore_signal(barrier, inc=1, device_id={"dp": (me + k) % n}, device_id_type=MESH)
+        return carry
+
+    lax.fori_loop(1, n, greet, 0)
+    pl.semaphore_wait(barrier, n - 1)
+
+    def remote(src, dst, ss, rs, target):
+        return pltpu.make_async_remote_copy(
+            src_ref=src, dst_ref=dst, send_sem=ss, recv_sem=rs,
+            device_id={"dp": target}, device_id_type=MESH,
+        )
+
+    def stat_copy(k):
+        peer = (me + k) % n
+        return remote(st_ref.at[peer], st_in.at[k], st_ss.at[k], st_rs.at[k], peer)
+
+    def pair_copy(j):
+        return remote(pair_out.at[j], pair_in.at[j], pair_ss.at[j], pair_rs.at[j], twin)
+
+    def ahead(owner):
+        up = owner > place
+        nearer = jnp.where(up, place + 1, place - 1)
+        slot = jnp.where(jnp.logical_and(owner == nearer, jnp.logical_not(up)), length, owner)
+        return nearer * 2 + side, slot
+
+    def line_copy(owner, target, slot):
+        return remote(own.at[owner], line_in.at[slot], line_ss.at[owner], line_rs.at[slot], target)
+
+    def lineb_copy(owner, target, slot):
+        return remote(own_b.at[owner], line_in_b.at[slot], lineb_ss.at[owner], lineb_rs.at[slot], target)
+
+    def swap_copy():
+        return remote(
+            own_b.at[place, pl.ds((1 - side) * rows, rows)], swap_in, swap_ss.at[0], swap_rs.at[0], twin
+        )
+
+    def flow(owner, copy, buffer, landed):
+        up = owner > place
+        mine = owner == place
+        from_low = jnp.logical_and(jnp.logical_or(up, mine), place > 0)
+        from_high = jnp.logical_and(jnp.logical_not(up), place < length - 1)
+
+        def take(slot):
+            copy(slot % length, twin, slot).wait_recv()
+            buffer[owner] = buffer[owner] + landed[slot]
+
+        @pl.when(from_low)
+        def _():
+            take(owner)
+
+        @pl.when(from_high)
+        def _():
+            take(jnp.where(mine, length, owner))
+
+        @pl.when(jnp.logical_not(mine))
+        def _():
+            target, slot = ahead(owner)
+            copy(owner, target, slot).start()
+
+    def first_pass(j, carry):
+        owner = owner_at(place, length, j)
+
+        def product(block, narrow_row):
+            own_b[owner, pl.ds(narrow_row, rows)] = jnp.dot(
+                x_ref[block], y_ref[:, wide:total], preferred_element_type=jnp.float32
+            )
+            return jnp.dot(x_ref[block], y_ref[:, 0:wide], preferred_element_type=jnp.float32)
+
+        pair_out[j] = product(owner * 2 + (1 - side), (1 - side) * rows)
+
+        @pl.when(j == 0)
+        def _():
+            pair_copy(j).start()
+
+        own[owner] = product(owner * 2 + side, side * rows)
+        flow(owner, lineb_copy, own_b, line_in_b)
+        return carry
+
+    lax.fori_loop(0, length, first_pass, 0)
+
+    def second_pass(j, carry):
+        owner = owner_at(place, length, j)
+        pair_copy(j).wait()
+
+        @pl.when(j < length - 1)
+        def _():
+            pair_copy(j + 1).start()
+
+        @pl.when(j == length - 1)
+        def _():
+            swap_copy().start()
+
+        @pl.when(j == 0)
+        def _():
+            def push(k, inner):
+                stat_copy(k).start()
+                return inner
+
+            lax.fori_loop(1, n, push, 0)
+
+        own[owner] = own[owner] + pair_in[j]
+        flow(owner, line_copy, own, line_in)
+        return carry
+
+    lax.fori_loop(0, length, second_pass, 0)
+    out_ref[:, 0:wide] = own[place]
+    swap_copy().wait()
+    out_ref[:, wide:total] = own_b[place, pl.ds(side * rows, rows)] + swap_in[...]
+
+    def settle(k, carry):
+        stat_copy(k).wait()
+        stats_ref[k] = st_in[k]
+        return carry
+
+    lax.fori_loop(1, n, settle, 0)
+    stats_ref[0] = st_ref[me]
+
+    def drain(owner, carry):
+        @pl.when(owner != place)
+        def _():
+            lineb_copy(owner, twin, owner).wait_send()
+            line_copy(owner, twin, owner).wait_send()
+
+        return carry
+
+    lax.fori_loop(0, length, drain, 0)
+
+
+def reduce_blocks(blocks, columns, packed):
+    n, rows, depth = blocks.shape
+    total = columns.shape[1]
+    narrow = max(128, total // 8 // 128 * 128)
+    wide = total - narrow
+    length = n // 2
+    dma = pltpu.SemaphoreType.DMA
+    f32 = jnp.float32
+    vmem = pl.BlockSpec(memory_space=pltpu.VMEM)
+    return pl.pallas_call(
+        functools.partial(reduce_kernel, n),
+        out_shape=(
+            jax.ShapeDtypeStruct((rows, total), f32),
+            jax.ShapeDtypeStruct(packed.shape, f32),
+        ),
+        in_specs=[vmem] * 3,
+        out_specs=(vmem, vmem),
+        scratch_shapes=[
+            pltpu.VMEM((length, rows, wide), f32),
+            pltpu.VMEM((length, rows, wide), f32),
+            pltpu.VMEM((length, rows, wide), f32),
+            pltpu.VMEM((length + 1, rows, wide), f32),
+            pltpu.VMEM((length, 2 * rows, narrow), f32),
+            pltpu.VMEM((length + 1, 2 * rows, narrow), f32),
+            pltpu.VMEM((rows, narrow), f32),
+            pltpu.VMEM(packed.shape, f32),
+            dma((length,)), dma((length,)),
+            dma((length,)), dma((length + 1,)),
+            dma((length,)), dma((length + 1,)),
+            dma((1,)), dma((1,)),
+            dma((n,)), dma((n,)),
+        ],
+        name="reduce_blocks",
+        compiler_params=pltpu.CompilerParams(
+            collective_id=0, has_side_effects=True, vmem_limit_bytes=60 * 1024 * 1024
+        ),
+    )(blocks, columns, packed)
 
 
 def per_device(view_first, view_second, valid_rows):
@@ -30,33 +227,32 @@
     square_second = jnp.sum(jnp.square(centered_second.astype(jnp.float32)), axis=0)
     group_index = lax.axis_index("dp")
     row_start = group_index * block_rows
-    counts_all, sums_first, sums_second, squares_first, squares_second = (
-        lax.all_gather(used_float[None], "dp", axis=0, tiled=True),
-        lax.all_gather(sum_first[None], "dp", axis=0, tiled=True),
-        lax.all_gather(sum_second[None], "dp", axis=0, tiled=True),
-        lax.all_gather(square_first[None], "dp", axis=0, tiled=True),
-        lax.all_gather(square_second[None], "dp", axis=0, tiled=True),
-    )
-    moment = lax.psum_scatter(
-        lax.dot_general(
-            centered_first,
-            centered_second,
-            (((0,), (0,)), ((), ())),
-            preferred_element_type=jnp.float32,
-        ),
-        "dp",
-        scatter_dimension=0,
-        tiled=True,
-    )
-    counts_col = counts_all[:, None]
-    all_rows = jnp.sum(counts_all)
-    glob_first = jnp.sum(sums_first, axis=0) / all_rows
+    shared = jnp.concatenate([sum_second, square_second, used_float[None]])
+    packed = jnp.concatenate(
+        [
+            sum_first.reshape(group_count, block_rows),
+            square_first.reshape(group_count, block_rows),
+            jnp.broadcast_to(shared[None], (group_count, shared.shape[0])),
+        ],
+        axis=1,
+    )
+    filled = packed.shape[1]
+    packed = jnp.pad(packed, ((0, 0), (0, -filled % 1024))).reshape(group_count, -1, 128)
+    blocks = jnp.transpose(centered_first).reshape(group_count, block_rows, local_rows)
+    moment, stats = reduce_blocks(blocks, centered_second, packed)
+    stats = stats.reshape(group_count, -1)
+    cuts = [block_rows, 2 * block_rows, 2 * block_rows + column_width, 2 * block_rows + 2 * column_width]
+    sums_rows = stats[:, : cuts[0]]
+    squares_rows = stats[:, cuts[0] : cuts[1]]
+    sums_second = stats[:, cuts[1] : cuts[2]]
+    squares_second = stats[:, cuts[2] : cuts[3]]
+    counts_col = stats[:, cuts[3] : cuts[3] + 1]
+    all_rows = jnp.sum(counts_col)
+    glob_rows = jnp.sum(sums_rows, axis=0) / all_rows
     glob_second = jnp.sum(sums_second, axis=0) / all_rows
-    shifts_first = sums_first / counts_col - glob_first[None, :]
+    owned_shift = sums_rows / counts_col - glob_rows[None, :]
     shifts_second = sums_second / counts_col - glob_second[None, :]
-    owned_shift = lax.dynamic_slice_in_dim(shifts_first, row_start, block_rows, 1)
-    owned_square = lax.dynamic_slice_in_dim(squares_first, row_start, block_rows, 1)
-    spread_rows = jnp.sum(owned_square + counts_col * jnp.square(owned_shift), axis=0)
+    spread_rows = jnp.sum(squares_rows + counts_col * jnp.square(owned_shift), axis=0)
     spread_second = jnp.sum(squares_second + counts_col * jnp.square(shifts_second), axis=0)
     weighted = owned_shift * counts_col
     moment = moment + lax.dot_general(

time: 368 us -> 266 us (0.72)
  Pallas kernels: 0 us -> 182 us
  blocking collectives: 192 us -> 41.5 us
  waiting for transfers between devices: 120 us -> 0 us
  between operations: 16.6 us -> 3.17 us
  matrix products: 24 us -> 11 us
  local copies, waits for them, and re-layouts: 3.39 us -> 13.9 us
    pallas_call x0 -> x1, Pallas kernels: none -> 182 us  [reduce_blocks(): pl.pallas_call(functools.partial(reduce_kernel, n), out_shape=(jax.ShapeD...]
    all_gather x4 -> x0, blocking collectives: 128 us -> none  [the longest x1 32.6 us: per_device(): lax.all_gather(square_first[None], 'dp', axis=0, tiled=True)]
    reduce_scatter x1 -> x0, waiting for transfers between devices: 120 us -> none  [per_device(): lax.psum_scatter(lax.dot_general(centered_first, centered_second, (((0,),...]
    unnamed x1 -> x0, blocking collectives: 24.4 us -> none
    dot_general x1 -> x0, matrix products: 12.8 us -> none  [per_device(): lax.dot_general(centered_first, centered_second, (((0,), (0,)), ((), ()))...]
    transpose x0 -> x1, local copies, waits for them, and re-layouts: none -> 12.1 us  [per_device(): jnp.transpose(centered_first).reshape(group_count, block_rows, local_rows)]
  transfers between devices with their start and end apart: 1 -> 0, of which waited for: 1 -> 0; matrix products, arithmetic and copies ran while one was open for 3% -> 0% of each run, Pallas kernels for 0% -> 0%
where the time goes in v1:
time: 266 us
  Pallas kernels  182 us (68%)
  blocking collectives  41.5 us (16%)
  other arithmetic  14.2 us (5%)
  local copies, waits for them, and re-layouts  13.9 us (5%)
  matrix products  11 us (4%)
  between operations  3.17 us (1%)
    pallas_call x1, Pallas kernels, reduce_blocks(): pl.pallas_call(functools.partial(reduce_kernel, n), out_shape=(jax.ShapeD...  182 us
    psum x1, blocking collectives, per_device(): loss = lax.psum(partial_loss, ('dp', 'col')) / feature_width  41.5 us
    transpose x1, local copies, waits for them, and re-layouts, per_device(): jnp.transpose(centered_first).reshape(group_count, block_rows, local_rows)  12.1 us
    reduce_sum x1, other arithmetic, per_device(): jnp.sum(jnp.square(centered_first.astype(jnp.float32)), axis=0)  8.6 us
    dot_general x1, matrix products, per_device(): lax.dot_general(weighted, shifts_second, (((0,), (0,)), ((), ())), precis...  6.06 us

profile of v1, /device:TPU:0, one launch (start us, length us, event | category | flops | bytes accessed | tf_op | source)
XLA Modules:
  0.0 265.7 jit_solution(14703481286240393106)
XLA Ops:
  1.3 4.6 %fusion.7 = f32[1,4096]{1,0:T(1,128)S(1)} fusion(bf16[1024,1]{0,1:T(2,128)(2,1)S(1)} %reshape.73, bf16[1024,4096]{1,0:T(8,128)(2,1)} %param.3), kind=kOutput, calls=%fused_computation.35 | convolution fusion | flops 8388608 | bytes 8407040 | tf_op jit(solution)/shard_map/dot_general | solution.py:218
  5.9 8.6 %multiply_reduce_fusion = (f32[4096]{0:T(1024)S(1)}, bf16[4096,1024]{0,1:T(8,128)(2,1)}) fusion(f32[1024]{0:T(1024)S(1)} %get-tuple-element.14, f32[4096]{0:T(1024)S(1)} %broadcast_divide_fusion, bf16[1024,4096]{1,0:T(8,128)(2,1)} %param.3), kind=kLoop, calls=%fused_computation | loop fusion | flops 29356032 | bytes 16814080 | tf_op jit(solution)/shard_map/reduce_sum | solution.py:226
  14.5 0.0 copy-start
  14.5 12.1 %copy.5 = bf16[4096,1024]{1,0:T(8,128)(2,1)} copy(bf16[4096,1024]{0,1:T(8,128)(2,1)} %get-tuple-element.9) | data formatting | bytes 16777216 | tf_op jit(solution)/shard_map/transpose | solution.py:241
  26.6 0.0 copy-done
  26.6 0.4 fusion.8
  27.0 2.1 multiply_reduce_fusion.1
  29.2 0.7 copy.14
  29.8 182.0 %reduce_blocks.1 = (f32[512,1024]{1,0:T(8,128)}, f32[8,32,128]{2,1,0:T(8,128)}) custom-call(bf16[8,512,1024]{2,1,0:T(8,128)(2,1)} %bitcast.23, bf16[1024,1024]{1,0:T(8,128)(2,1)} %get-tuple-element.7.y_ref, f32[8,32,128]{2,1,0:T(8,128)} %bitcast.30), custom_call_target="tpu_custom_call" | custom-call | tf_op jit(solution)/shard_map/reduce_blocks/pallas_call | solution.py:177
  211.9 1.0 copy.13
  212.8 0.6 slice_reduce_fusion.2
  213.4 0.1 copy.7
  213.5 0.7 broadcast_divide_fusion.1
  214.2 0.1 fusion.1
  214.3 0.7 add_sqrt_fusion
  215.0 0.7 broadcast_divide_fusion.3
  215.6 0.1 fusion.2
  215.7 0.7 sqrt_multiply_fusion
  216.4 6.1 %select_reduce_fusion = (f32[]{:T(128)}, f32[512,1024]{1,0:T(8,128)}) fusion(s32[1024]{0:T(1024)S(1)} %iota_add_fusion, s32[512]{0:T(512)S(1)} %iota_add_fusion.1, f32[1024]{0:T(1024)S(1)} %add_sqrt_fusion, f32[512]{0:T(512)S(1)} %sqrt_multiply_fusion, f32[512,1024]{1,0:T(8,128)} %get-tuple-element.4, f32[8,4096]{1,0:T(8,128)S(1)} %bitcast.29, ...), kind=kOutput, calls=%fused_computation.5 | convolution fusion | flops 55603200 | bytes 4262916 | tf_op jit(solution)/shard_map/dot_general | solution.py:258
  222.4 41.5 %psum.7 = f32[]{:T(128)} all-reduce(f32[]{:T(128)} %get-tuple-element.12), channel_id=1, replica_groups=mesh['dp'=8,'col'=4] {'dp','col'}, use_global_device_ids=true, to_apply=%region_8.9 | all-reduce | flops 1 | bytes 8 | tf_op jit(solution)/shard_map/psum | solution.py:274
  (13 shorter events, 0.1 us)
Async XLA Ops:
  14.5 12.1 %copy-start = (bf16[1024,1024]{1,0:T(8,128)(2,1)S(1)}, bf16[1024,1024]{1,0:T(8,128)(2,1)}, u32[]{:S(2)}) copy-start(bf16[1024,1024]{1,0:T(8,128)(2,1)} %param.4) | copy-start | bytes 6291460

commit v2 on v1

--- a/solution.py
+++ b/solution.py
@@ -22,16 +22,17 @@
 
 
 def reduce_kernel(
-    n, x_ref, y_ref, st_ref, out_ref, stats_ref,
-    pair_out, own, pair_in, line_in, own_b, line_in_b, swap_in, st_in,
-    pair_ss, pair_rs, line_ss, line_rs, lineb_ss, lineb_rs, swap_ss, swap_rs, st_ss, st_rs,
+    n, x_ref, y_ref, sum_ref, tail_ref, out_ref, first_ref, second_ref,
+    terms, pair_in, line_in, own_b, line_in_b, swap_in, sf, sy, sf_in, sy_in,
+    pair_ss, pair_rs, line_ss, line_rs, lineb_ss, lineb_rs, swap_ss, swap_rs,
+    sf_ss, sf_rs, sy_ss, sy_rs,
 ):
     me = lax.axis_index("dp")
     length = n // 2
     place, side = me // 2, me % 2
     twin = place * 2 + (1 - side)
-    rows = x_ref.shape[1]
-    wide = own.shape[2]
+    rows = terms.shape[2]
+    wide = terms.shape[3]
     total = y_ref.shape[1]
 
     barrier = pltpu.get_barrier_semaphore()
@@ -49,12 +50,16 @@
             device_id={"dp": target}, device_id_type=MESH,
         )
 
-    def stat_copy(k):
+    def first_copy(k):
         peer = (me + k) % n
-        return remote(st_ref.at[peer], st_in.at[k], st_ss.at[k], st_rs.at[k], peer)
+        return remote(sf.at[peer // 2], sf_in.at[k], sf_ss.at[k], sf_rs.at[k], peer)
+
+    def second_copy(k):
+        return remote(sy, sy_in.at[k], sy_ss.at[k], sy_rs.at[k], (me + k) % n)
 
     def pair_copy(j):
-        return remote(pair_out.at[j], pair_in.at[j], pair_ss.at[j], pair_rs.at[j], twin)
+        source = terms.at[owner_at(place, length, j), 1 - side]
+        return remote(source, pair_in.at[j], pair_ss.at[j], pair_rs.at[j], twin)
 
     def ahead(owner):
         up = owner > place
@@ -63,7 +68,7 @@
         return nearer * 2 + side, slot
 
     def line_copy(owner, target, slot):
-        return remote(own.at[owner], line_in.at[slot], line_ss.at[owner], line_rs.at[slot], target)
+        return remote(terms.at[owner, side], line_in.at[slot], line_ss.at[owner], line_rs.at[slot], target)
 
     def lineb_copy(owner, target, slot):
         return remote(own_b.at[owner], line_in_b.at[slot], lineb_ss.at[owner], lineb_rs.at[slot], target)
@@ -73,7 +78,7 @@
             own_b.at[place, pl.ds((1 - side) * rows, rows)], swap_in, swap_ss.at[0], swap_rs.at[0], twin
         )
 
-    def flow(owner, copy, buffer, landed):
+    def flow(owner, copy, at, buffer, landed):
         up = owner > place
         mine = owner == place
         from_low = jnp.logical_and(jnp.logical_or(up, mine), place > 0)
@@ -81,7 +86,7 @@
 
         def take(slot):
             copy(slot % length, twin, slot).wait_recv()
-            buffer[owner] = buffer[owner] + landed[slot]
+            buffer[at] = buffer[at] + landed[slot]
 
         @pl.when(from_low)
         def _():
@@ -99,23 +104,34 @@
     def first_pass(j, carry):
         owner = owner_at(place, length, j)
 
-        def product(block, narrow_row):
-            own_b[owner, pl.ds(narrow_row, rows)] = jnp.dot(
-                x_ref[block], y_ref[:, wide:total], preferred_element_type=jnp.float32
+        start = pl.multiple_of(owner * (2 * rows), 2 * rows)
+        pair = x_ref[:, pl.ds(start, 2 * rows)]
+
+        def product(low, high):
+            return lax.dot_general(
+                pair, y_ref[:, low:high], (((0,), (0,)), ((), ())),
+                preferred_element_type=jnp.float32,
             )
-            return jnp.dot(x_ref[block], y_ref[:, 0:wide], preferred_element_type=jnp.float32)
-
-        pair_out[j] = product(owner * 2 + (1 - side), (1 - side) * rows)
+
+        both = product(0, wide)
+        terms[owner, 0] = both[:rows]
+        terms[owner, 1] = both[rows:]
 
         @pl.when(j == 0)
         def _():
             pair_copy(j).start()
 
-        own[owner] = product(owner * 2 + side, side * rows)
-        flow(owner, lineb_copy, own_b, line_in_b)
+        own_b[owner] = product(wide, total)
+        squares = jnp.sum(jnp.square(pair.astype(jnp.float32)), axis=0, keepdims=True)
+        line = lax.broadcasted_iota(jnp.int32, (8, 2 * rows), 0)
+        sf[owner] = jnp.where(line == 0, sum_ref[owner], squares)
+        flow(owner, lineb_copy, owner, own_b, line_in_b)
         return carry
 
     lax.fori_loop(0, length, first_pass, 0)
+    squares = jnp.sum(jnp.square(y_ref[...].astype(jnp.float32)), axis=0, keepdims=True)
+    line = lax.broadcasted_iota(jnp.int32, (8, total), 0)
+    sy[...] = jnp.where(line == 0, tail_ref[0:1], jnp.where(line == 1, squares, tail_ref[1:2]))
 
     def second_pass(j, carry):
         owner = owner_at(place, length, j)
@@ -132,27 +148,31 @@
         @pl.when(j == 0)
         def _():
             def push(k, inner):
-                stat_copy(k).start()
+                first_copy(k).start()
+                second_copy(k).start()
                 return inner
 
             lax.fori_loop(1, n, push, 0)
 
-        own[owner] = own[owner] + pair_in[j]
-        flow(owner, line_copy, own, line_in)
+        terms[owner, side] = terms[owner, side] + pair_in[j]
+        flow(owner, line_copy, (owner, side), terms, line_in)
         return carry
 
     lax.fori_loop(0, length, second_pass, 0)
-    out_ref[:, 0:wide] = own[place]
+    out_ref[:, 0:wide] = terms[place, side]
     swap_copy().wait()
     out_ref[:, wide:total] = own_b[place, pl.ds(side * rows, rows)] + swap_in[...]
 
     def settle(k, carry):
-        stat_copy(k).wait()
-        stats_ref[k] = st_in[k]
+        first_copy(k).wait()
+        second_copy(k).wait()
+        first_ref[k] = sf_in[k]
+        second_ref[k] = sy_in[k]
         return carry
 
     lax.fori_loop(1, n, settle, 0)
-    stats_ref[0] = st_ref[me]
+    first_ref[0] = sf[place]
+    second_ref[0] = sy[...]
 
     def drain(owner, carry):
         @pl.when(owner != place)
@@ -165,8 +185,8 @@
     lax.fori_loop(0, length, drain, 0)
 
 
-def reduce_blocks(blocks, columns, packed):
-    n, rows, depth = blocks.shape
+def reduce_blocks(n, first, columns, sums, tail):
+    rows = first.shape[1] // n
     total = columns.shape[1]
     narrow = max(128, total // 8 // 128 * 128)
     wide = total - narrow
@@ -178,30 +198,96 @@
         functools.partial(reduce_kernel, n),
         out_shape=(
             jax.ShapeDtypeStruct((rows, total), f32),
-            jax.ShapeDtypeStruct(packed.shape, f32),
+            jax.ShapeDtypeStruct((n, 8, 2 * rows), f32),
+            jax.ShapeDtypeStruct((n, 8, total), f32),
         ),
-        in_specs=[vmem] * 3,
-        out_specs=(vmem, vmem),
+        in_specs=[vmem] * 4,
+        out_specs=(vmem, vmem, vmem),
         scratch_shapes=[
-            pltpu.VMEM((length, rows, wide), f32),
-            pltpu.VMEM((length, rows, wide), f32),
+            pltpu.VMEM((length, 2, rows, wide), f32),
             pltpu.VMEM((length, rows, wide), f32),
             pltpu.VMEM((length + 1, rows, wide), f32),
             pltpu.VMEM((length, 2 * rows, narrow), f32),
             pltpu.VMEM((length + 1, 2 * rows, narrow), f32),
             pltpu.VMEM((rows, narrow), f32),
-            pltpu.VMEM(packed.shape, f32),
+            pltpu.VMEM((length, 8, 2 * rows), f32),
+            pltpu.VMEM((8, total), f32),
+            pltpu.VMEM((n, 8, 2 * rows), f32),
+            pltpu.VMEM((n, 8, total), f32),
             dma((length,)), dma((length,)),
             dma((length,)), dma((length + 1,)),
             dma((length,)), dma((length + 1,)),
             dma((1,)), dma((1,)),
-            dma((n,)), dma((n,)),
+            dma((n,)), dma((n,)), dma((n,)), dma((n,)),
         ],
         name="reduce_blocks",
         compiler_params=pltpu.CompilerParams(
             collective_id=0, has_side_effects=True, vmem_limit_bytes=60 * 1024 * 1024
         ),
-    )(blocks, columns, packed)
+    )(first, columns, sums, tail)
+
+
+def total_kernel(n, m, part_ref, out_ref, held, line, across, ss, rs, ss2, rs2):
+    me, col = lax.axis_index("dp"), lax.axis_index("col")
+    barrier = pltpu.get_barrier_semaphore()
+
+    def each(count, body):
+        def step(k, carry):
+            body(k)
+            return carry
+
+        lax.fori_loop(1, count, step, 0)
+
+    def greet(axis, index, count):
+        return lambda k: pl.semaphore_signal(
+            barrier, inc=1, device_id={axis: (index + k) % count}, device_id_type=MESH
+        )
+
+    each(n, greet("dp", me, n))
+    each(m, greet("col", col, m))
+    pl.semaphore_wait(barrier, n + m - 2)
+
+    def dp_copy(k):
+        return pltpu.make_async_remote_copy(
+            src_ref=part_ref, dst_ref=line.at[me], send_sem=ss.at[k], recv_sem=rs.at[k],
+            device_id={"dp": (me + k) % n}, device_id_type=MESH,
+        )
+
+    def col_copy(k):
+        return pltpu.make_async_remote_copy(
+            src_ref=held, dst_ref=across.at[col], send_sem=ss2.at[k], recv_sem=rs2.at[k],
+            device_id={"col": (col + k) % m}, device_id_type=MESH,
+        )
+
+    each(n, lambda k: dp_copy(k).start())
+    line[me] = part_ref[...]
+    each(n, lambda k: dp_copy(k).wait())
+    held[...] = jnp.sum(line[...], axis=0)
+    each(m, lambda k: col_copy(k).start())
+    across[col] = held[...]
+    each(m, lambda k: col_copy(k).wait())
+    out_ref[...] = jnp.sum(across[...], axis=0)
+
+
+def add_everywhere(n, m, value):
+    f32 = jnp.float32
+    vmem = pl.BlockSpec(memory_space=pltpu.VMEM)
+    dma = pltpu.SemaphoreType.DMA
+    tile = (8, 128)
+    return pl.pallas_call(
+        functools.partial(total_kernel, n, m),
+        out_shape=jax.ShapeDtypeStruct(tile, f32),
+        in_specs=[vmem],
+        out_specs=vmem,
+        scratch_shapes=[
+            pltpu.VMEM(tile, f32),
+            pltpu.VMEM((n,) + tile, f32),
+            pltpu.VMEM((m,) + tile, f32),
+            dma((n,)), dma((n,)), dma((m,)), dma((m,)),
+        ],
+        name="add_everywhere",
+        compiler_params=pltpu.CompilerParams(collective_id=1, has_side_effects=True),
+    )(jnp.broadcast_to(value, tile))[0, 0]
 
 
 def per_device(view_first, view_second, valid_rows):
@@ -223,30 +309,19 @@
     centered_second = ((view_second.astype(jnp.float32) - mean_second) * live_col).astype(
         jnp.bfloat16
     )
-    square_first = jnp.sum(jnp.square(centered_first.astype(jnp.float32)), axis=0)
-    square_second = jnp.sum(jnp.square(centered_second.astype(jnp.float32)), axis=0)
     group_index = lax.axis_index("dp")
     row_start = group_index * block_rows
-    shared = jnp.concatenate([sum_second, square_second, used_float[None]])
-    packed = jnp.concatenate(
-        [
-            sum_first.reshape(group_count, block_rows),
-            square_first.reshape(group_count, block_rows),
-            jnp.broadcast_to(shared[None], (group_count, shared.shape[0])),
-        ],
-        axis=1,
-    )
-    filled = packed.shape[1]
-    packed = jnp.pad(packed, ((0, 0), (0, -filled % 1024))).reshape(group_count, -1, 128)
-    blocks = jnp.transpose(centered_first).reshape(group_count, block_rows, local_rows)
-    moment, stats = reduce_blocks(blocks, centered_second, packed)
-    stats = stats.reshape(group_count, -1)
-    cuts = [block_rows, 2 * block_rows, 2 * block_rows + column_width, 2 * block_rows + 2 * column_width]
-    sums_rows = stats[:, : cuts[0]]
-    squares_rows = stats[:, cuts[0] : cuts[1]]
-    sums_second = stats[:, cuts[1] : cuts[2]]
-    squares_second = stats[:, cuts[2] : cuts[3]]
-    counts_col = stats[:, cuts[3] : cuts[3] + 1]
+    tail = jnp.stack([sum_second, jnp.broadcast_to(used_float, sum_second.shape)])
+    sums = sum_first.reshape(group_count // 2, 1, 2 * block_rows)
+    moment, stats_first, stats_second = reduce_blocks(
+        group_count, centered_first, centered_second, sums, tail
+    )
+    stats_first = lax.dynamic_slice_in_dim(
+        stats_first[:, :2], group_index % 2 * block_rows, block_rows, 2
+    )
+    sums_rows, squares_rows = stats_first[:, 0], stats_first[:, 1]
+    sums_second, squares_second = stats_second[:, 0], stats_second[:, 1]
+    counts_col = stats_second[:, 2, :1]
     all_rows = jnp.sum(counts_col)
     glob_rows = jnp.sum(sums_rows, axis=0) / all_rows
     glob_second = jnp.sum(sums_second, axis=0) / all_rows
@@ -271,7 +346,7 @@
     diagonal = global_rows == global_cols
     terms = jnp.where(diagonal, jnp.square(1.0 - correlation), off_weight * jnp.square(correlation))
     partial_loss = jnp.sum(terms)
-    loss = lax.psum(partial_loss, ("dp", "col")) / feature_width
+    loss = add_everywhere(group_count, lax.axis_size("col"), partial_loss) / feature_width
     return (correlation, loss)
 
 

time: 266 us -> 238 us (0.89)
  blocking collectives: 41.5 us -> 0 us
  Pallas kernels: 182 us -> 201 us
  local copies, waits for them, and re-layouts: 13.9 us -> 6.09 us
    psum x1 -> x0, blocking collectives: 41.5 us -> none  [per_device(): loss = lax.psum(partial_loss, ('dp', 'col')) / feature_width]
    pallas_call x0 -> x1, Pallas kernels: none -> 14.2 us  [add_everywhere(): pl.pallas_call(functools.partial(total_kernel, n, m), out_shape=jax.Shape...]
    convert_element_type x0 -> x2, other arithmetic: none -> 12.3 us  [the longest x1 10.4 us: per_device(): ((view_first.astype(jnp.float32) - mean_first) * live_col).astype(jnp.bfl...]
    transpose x1 -> x0, local copies, waits for them, and re-layouts: 12.1 us -> none  [per_device(): jnp.transpose(centered_first).reshape(group_count, block_rows, local_rows)]
    reduce_sum x3 -> x0, other arithmetic: 11.3 us -> none  [the longest x1 8.6 us: per_device(): jnp.sum(jnp.square(centered_first.astype(jnp.float32)), axis=0)]
    pallas_call x1, Pallas kernels: 182 us -> 187 us  [reduce_blocks(): pl.pallas_call(functools.partial(reduce_kernel, n), out_shape=(jax.ShapeD...]
    slice x0 -> x3, local copies, waits for them, and re-layouts: none -> 3.13 us  [the longest x1 1.18 us: add_everywhere(): pl.pallas_call(functools.partial(total_kernel, n, m), out_shape=jax.Shape...]
where the time goes in v2:
time: 238 us
  Pallas kernels  201 us (84%)
  other arithmetic  16.7 us (7%)
  matrix products  11 us (5%)
  local copies, waits for them, and re-layouts  6.09 us (3%)
  between operations  3.19 us (1%)
    pallas_call x1, Pallas kernels, reduce_blocks(): pl.pallas_call(functools.partial(reduce_kernel, n), out_shape=(jax.ShapeD...  187 us
    pallas_call x1, Pallas kernels, add_everywhere(): pl.pallas_call(functools.partial(total_kernel, n, m), out_shape=jax.Shape...  14.2 us
    convert_element_type x1, other arithmetic, per_device(): ((view_first.astype(jnp.float32) - mean_first) * live_col).astype(jnp.bfl...  10.4 us
    dot_general x1, matrix products, per_device(): lax.dot_general(weighted, shifts_second, (((0,), (0,)), ((), ())), precis...  6.06 us

profile of v2, /device:TPU:0, one launch (start us, length us, event | category | flops | bytes accessed | tf_op | source)
XLA Modules:
  0.0 237.9 jit_solution(1105426828713555038)
XLA Ops:
  1.3 4.6 %fusion.24 = f32[1,4096]{1,0:T(1,128)S(1)} fusion(bf16[1024,1]{0,1:T(2,128)(2,1)S(1)} %reshape.96, bf16[1024,4096]{1,0:T(8,128)(2,1)} %param.3), kind=kOutput, calls=%fused_computation.46 | convolution fusion | flops 8388608 | bytes 8407040 | tf_op jit(solution)/shard_map/dot_general | solution.py:304
  5.9 0.0 copy-start.1
  5.9 0.0 copy-start
  5.9 10.4 %multiply_convert_fusion.x_ref = bf16[1024,4096]{1,0:T(8,128)(2,1)} fusion(bf16[1024,4096]{1,0:T(8,128)(2,1)} %param.3, f32[1024]{0:T(1024)S(1)} %get-tuple-element.15, f32[4096]{0:T(1024)S(1)} %broadcast_divide_fusion), kind=kLoop, calls=%fused_computation | loop fusion | flops 16777216 | bytes 16797696 | tf_op jit(solution)/shard_map/convert_element_type | solution.py:308
  16.3 0.0 copy-done.1
  16.3 0.0 copy-done
  16.3 0.4 fusion.25
  16.7 1.8 multiply_convert_fusion.1.y_ref
  18.6 0.6 stack.3.tail_ref
  19.2 186.7 %reduce_blocks.1 = (f32[512,1024]{1,0:T(8,128)}, f32[8,8,1024]{2,1,0:T(8,128)}, f32[8,8,1024]{2,1,0:T(8,128)}) custom-call(bf16[1024,4096]{1,0:T(8,128)(2,1)} %multiply_convert_fusion.x_ref, bf16[1024,1024]{1,0:T(8,128)(2,1)} %multiply_convert_fusion.1.y_ref, f32[4,1,1024]{2,1,0:T(1,128)} %bitcast.51, f32[2,1024]{1,0:T(2,128)} %stack.3.tail_ref), custom_call_target="tpu_custom_call" | custom-call | tf_op jit(solution)/shard_map/reduce_blocks/pallas_call | solution.py:197
  205.9 1.0 slice.21
  206.9 0.1 fusion.23
  207.0 1.5 slice_reduce_fusion.2
  208.5 0.6 broadcast_divide_fusion.3
  209.2 0.1 fusion.8
  209.2 0.7 sqrt_multiply_fusion
  209.9 1.1 copy.8
  211.0 0.7 broadcast_divide_fusion.1
  211.7 1.0 slice.26
  212.7 0.1 fusion
  212.8 0.7 add_sqrt_fusion
  213.5 6.1 %select_reduce_fusion = (f32[]{:T(128)}, f32[512,1024]{1,0:T(8,128)}) fusion(s32[1024]{0:T(1024)S(1)} %iota_add_fusion, s32[512]{0:T(512)S(1)} %iota_add_fusion.1, f32[1024]{0:T(1024)S(1)} %add_sqrt_fusion, f32[512]{0:T(512)S(1)} %sqrt_multiply_fusion, f32[512,1024]{1,0:T(8,128)} %get-tuple-element.5, f32[8,8,1024]{2,0,1:T(8,128)S(1)} %copy.8, ...), kind=kOutput, calls=%fused_computation.2 | convolution fusion | flops 55603200 | bytes 4262916 | tf_op jit(solution)/shard_map/dot_general | solution.py:333
  219.5 1.2 broadcast_in_dim.2.part_ref
  220.8 14.2 %add_everywhere.1 = f32[8,128]{1,0:T(8,128)} custom-call(f32[8,128]{1,0:T(8,128)} %broadcast_in_dim.2.part_ref), custom_call_target="tpu_custom_call" | custom-call | tf_op jit(solution)/shard_map/add_everywhere/pallas_call | solution.py:277
  234.9 1.2 slice.27
  (7 shorter events, 0.0 us)
Async XLA Ops:
  5.9 10.4 %copy-start.1 = (f32[1,4096]{1,0:T(1,128)}, f32[1,4096]{1,0:T(1,128)S(1)}, u32[]{:S(2)}) copy-start(f32[1,4096]{1,0:T(1,128)S(1)} %fusion.24) | copy-start | bytes 49156
  5.9 10.4 %copy-start = (bf16[1024,1024]{1,0:T(8,128)(2,1)S(1)}, bf16[1024,1024]{1,0:T(8,128)(2,1)}, u32[]{:S(2)}) copy-start(bf16[1024,1024]{1,0:T(8,128)(2,1)} %param.4) | copy-start | bytes 6291460
